TPU v7x, 32 devices: a whole 2x2x4 slice. The times are simulated.
32 devices in a mesh: pipe: 4 (over y, x), dp: 8 (over z, core).
Axes of the slice: x: 2, y: 2, z: 4, core: 2. Of those that a mesh axis runs over, the one named last changes fastest.
Arguments:
- acts: bfloat16 [4, 2048, 3072], P('pipe', 'dp'), may hold values from -24 to 24, as said below
- grad: float32 [12288, 4096], P('pipe', 'dp'), may hold values from -6 to 6
- owner_of: int32 [4, 12], replicated, may hold values from 0 to 3, as said below
Outputs:
- precond: float32 [12288, 4096], P('pipe', 'dp')
- held_inverse: float32 [4, 24, 256, 256], P('pipe', None, 'dp')
Inputs may be any that keep to these rules, and one draw needn't show every extreme that they name: `acts`: column and token scales of the activations vary; entries lie within the range. `owner_of`: no section index owns more than 24 blocks in all, and some section index owns exactly 24.
All inputs are finite; a program needn't handle non-finite values.
Results may differ from a plain program's by a relative error of at most 0.0003.
Values sent between devices are 32-bit elements; how exact they have to be, the bound alone decides.
A program may use at most 128 MiB of HBM per device.

v0:
```python
import jax
import jax.numpy as jnp
from jax import lax
from jax.sharding import PartitionSpec as P

BLK = 256
HOST = 24
damping_ratio = 0.1


def invert_blocks(factor, vacant):
    order_size = factor.shape[-1]
    diagonal_sum = jnp.sum(jnp.diagonal(factor, axis1=1, axis2=2), axis=1)
    damping = damping_ratio * diagonal_sum / order_size
    identity = jnp.eye(order_size, dtype=factor.dtype)
    shifted = factor + (damping + vacant)[:, None, None] * identity
    cholesky_lower = jnp.linalg.cholesky(shifted)
    identity_stack = jnp.broadcast_to(identity, factor.shape)
    inv_lower = lax.linalg.triangular_solve(
        cholesky_lower, identity_stack, left_side=True, lower=True
    )
    return jnp.einsum("mkr,mkc->mrc", inv_lower, inv_lower, precision=lax.Precision.HIGHEST)


def slot_tables(owner_of):
    owners_flat = owner_of.reshape(-1)
    positions = jnp.arange(owners_flat.shape[0], dtype=jnp.int32)
    matches = owners_flat[:, None] == owners_flat[None, :]
    before = positions[None, :] < positions[:, None]
    slot_rank = jnp.sum((matches & before).astype(jnp.int32), axis=1)
    return (owners_flat, slot_rank)


def shards(acts, grad, owner_of):
    tokens = acts.shape[1]
    feature_count = acts.shape[2]
    nblocks = feature_count // BLK
    data_count = lax.axis_size("dp")
    section_count = lax.axis_size("pipe")
    row_share = BLK // data_count
    all_tokens = tokens * data_count
    section_index = lax.axis_index("pipe")
    member = lax.axis_index("dp")
    features = acts[0].reshape(tokens, nblocks, BLK)
    owners_flat, slot_rank = slot_tables(owner_of)
    slot_ids = jnp.arange(HOST, dtype=jnp.int32)
    pick_mine = (
        (owners_flat[None, :] == section_index) & (slot_rank[None, :] == slot_ids[:, None])
    ).astype(jnp.float32)
    own_owners = lax.dynamic_index_in_dim(owner_of, section_index, 0, keepdims=False)
    own_ranks = lax.dynamic_index_in_dim(
        slot_rank.reshape(section_count, nblocks), section_index, 0, keepdims=False
    )
    target = own_owners * HOST + own_ranks
    pick_back = (
        jnp.arange(section_count * HOST, dtype=jnp.int32)[None, :] == target[:, None]
    ).astype(jnp.float32)
    block_terms = jnp.einsum("tbr,tbc->rbc", features, features, preferred_element_type=jnp.float32)
    my_rows = lax.psum_scatter(
        block_terms.reshape(row_share * lax.axis_size("dp"), nblocks * BLK),
        "dp",
        scatter_dimension=0,
        tiled=True,
    )
    pieces = lax.all_gather(my_rows, "pipe", axis=0, tiled=True).reshape(
        section_count, row_share, nblocks, BLK
    )
    hosted = jnp.einsum(
        "jsb,srbc->jrc",
        pick_mine.reshape(HOST, section_count, nblocks),
        pieces,
        precision=lax.Precision.HIGHEST,
    )
    occupied = jnp.sum(pick_mine, axis=1)
    per_member = (HOST + data_count - 1) // data_count
    padded_count = per_member * data_count
    padded = jnp.pad(hosted, ((0, padded_count - HOST), (0, 0), (0, 0)))
    mine_blocks = lax.all_to_all(padded, "dp", split_axis=0, concat_axis=1, tiled=True) / all_tokens
    padded_flags = jnp.pad(occupied, (0, padded_count - HOST))
    held_flags = lax.dynamic_slice_in_dim(padded_flags, member * per_member, per_member, 0)
    inverted = invert_blocks(mine_blocks, 1.0 - held_flags) * held_flags[:, None, None]
    spread_rows = lax.all_to_all(inverted, "dp", split_axis=1, concat_axis=0, tiled=True)
    held_rows = spread_rows[:HOST]
    returned = lax.all_gather(held_rows, "pipe", axis=0, tiled=True)
    own_rows = jnp.einsum("bm,mrc->brc", pick_back, returned, precision=lax.Precision.HIGHEST)
    inverse = lax.all_gather(own_rows, "dp", axis=1, tiled=True)
    grad_blocks = grad.reshape(nblocks, BLK, grad.shape[1])
    precond = jnp.einsum("brk,bkc->brc", inverse, grad_blocks, precision=lax.Precision.HIGHEST)
    return (precond.reshape(feature_count, grad.shape[1]), held_rows[None])


def solution(mesh):
    placed = (P("pipe", "dp", None), P("pipe", "dp"), P())
    return jax.shard_map(
        shards,
        mesh=mesh,
        in_specs=placed,
        out_specs=(P("pipe", "dp"), P("pipe", None, "dp", None)),
        check_vma=False,
    )
```

profile of v0, /device:TPU:0, one launch (start us, length us, event | category | flops | bytes accessed | tf_op | source)
XLA Modules:
  0.0 447.4 jit_solution(14781126711529102693)
XLA Ops:
  7.2 0.0 reduce-scatter.2.cloned.1.call-start
  7.2 1.7 copy.123
  8.9 2.3 fusion.30
  11.2 3.5 copy.125
  14.7 0.0 all-gather.4.cloned.1.call-start
  14.8 43.2 %reduce-scatter.2.cloned.1.call-done = f32[32,3072]{1,0:T(8,128)} async-done(((f32[256,3072]{1,0:T(8,128)}), f32[32,3072]{1,0:T(8,128)}) %reduce-scatter.2.cloned.1.call-update) | async-done | bytes 393232 | tf_op jit(solution)/shard_map/reduce_scatter | solution.py:59
  58.0 0.1 eq.76
  58.1 0.2 convert_reduce_fusion
  58.3 0.1 reshape.93
  58.4 31.6 %all-gather.4.cloned.1.call-done = f32[128,3072]{1,0:T(8,128)} async-done(((f32[32,3072]{1,0:T(8,128)}), f32[128,3072]{1,0:T(8,128)}) %all-gather.4.cloned.1.call-update) | async-done | bytes 1572880 | tf_op jit(solution)/shard_map/all_gather | solution.py:65
  90.0 1.7 reshape.95
  91.7 0.9 convolution_bitcast_fusion
  92.6 1.1 copy.127
  93.7 4.6 %all-to-all-start = ((f32[24,32,256]{2,1,0:T(8,128)}), f32[24,32,256]{2,1,0:T(8,128)S(1)}, u32[]{:S(2)}, u32[]{:S(2)}) async-start(f32[24,32,256]{2,1,0:T(8,128)} %copy.127), calls=%async_computation.1 | async-start | bytes 1572864 | tf_op jit(solution)/shard_map/all_to_all | solution.py:78
  98.3 0.2 all-gather.6.cloned.1.call-start
  98.6 0.7 copy.135
  99.4 0.1 copy.137
  99.5 0.5 iota_multiply_fusion
  100.0 0.1 convert_reduce_fusion.1
  100.1 0.6 iota_compare_fusion.2
  100.8 0.6 iota_compare_fusion.1
  101.4 17.8 %all-to-all-done = f32[24,32,256]{2,1,0:T(8,128)S(1)} async-done(((f32[24,32,256]{2,1,0:T(8,128)}), f32[24,32,256]{2,1,0:T(8,128)S(1)}, u32[]{:S(2)}, u32[]{:S(2)}) %all-to-all-start) | async-done | bytes 786464 | tf_op jit(solution)/shard_map/all_to_all | solution.py:78
  119.3 0.1 broadcast_multiply_fusion
  119.3 0.1 copy.128
  119.4 16.8 %copy.129 = f32[3,256,256]{0,2,1:T(8,128)} copy(f32[3,256,256]{2,1,0:T(8,128)S(1)} %bitcast.75) | data formatting | bytes 1572864 | tf_op jit(solution)/shard_map/div | solution.py:78
  136.2 0.3 copy.130
  136.5 2.3 gather_fusion
  138.8 0.1 reduce_sum.28
  138.9 0.6 subtract_add_fusion
  139.4 0.5 copy-done.4
  140.0 0.1 multiply_add_fusion
  140.1 0.3 copy.131
  140.4 0.8 fusion.5
  141.3 35.2 %custom-call.16 = f32[3,128,128]{2,1,0:T(8,128)S(1)} custom-call(f32[3,128,128]{2,1,0:T(8,128)S(1)} %cholesky.122), custom_call_target="Cholesky" | custom-call | tf_op jit(solution)/shard_map/jit(cholesky)/cholesky | solution.py:17
  176.4 0.1 cholesky.117
  176.5 0.8 select_bitcast_fusion
  177.3 29.5 %custom-call.17 = f32[3,1,128,128]{2,3,1,0:T(8,128)S(1)} custom-call(f32[3,1,128,128]{3,2,1,0:T(8,128)S(1)} %select_bitcast_fusion), custom_call_target="InvertDiagBlocksLowerTriangular" | custom-call | tf_op jit(solution)/shard_map/jit(cholesky)/cholesky | solution.py:17
  206.8 0.4 constant_dynamic-update-slice_fusion.1
  207.1 0.5 convolution_subtract_fusion.1
  207.7 35.4 %custom-call.18 = f32[3,128,128]{2,1,0:T(8,128)S(1)} custom-call(f32[3,128,128]{2,1,0:T(8,128)S(1)} %convolution_subtract_fusion.1), custom_call_target="Cholesky" | custom-call | tf_op jit(solution)/shard_map/jit(cholesky)/cholesky | solution.py:17
  243.1 0.1 compare_reduce_fusion
  243.3 0.2 select_select_fusion
  243.5 0.1 triangular_solve.69
  243.6 5.4 %while.1 = (s32[]{:T(128)}, f32[3,256,256]{2,1,0:T(8,128)S(1)}, s32[2,2]{1,0:T(2,128)S(1)}, f32[2,3,128,128]{3,2,0,1:T(8,128)}, s32[]{:T(128)}) while((s32[]{:T(128)}, f32[3,256,256]{2,1,0:T(8,128)S(1)}, s32[2,2]{1,0:T(2,128)S(1)}, f32[2,3,128,128]{3,2,0,1:T(8,128)}, s32[]{:T(128)}) %tuple.29), condition=%wide.while_cond, body=%wide.while_body.sunk | while | flops 2 | bytes 394849 | solution.py:19
  243.6 0.6 fusion.42
  244.2 2.1 bitcast_dynamic-update-slice_fusion.2
  246.2 0.6 fusion.42
  246.9 2.1 bitcast_dynamic-update-slice_fusion.2
  248.9 59.8 %custom-call.19 = f32[3,2,128,128]{2,3,1,0:T(8,128)S(1)} custom-call(f32[3,2,128,128]{3,2,1,0:T(8,128)} %bitcast.83), custom_call_target="InvertDiagBlocksLowerTriangular" | custom-call | tf_op jit(solution)/shard_map/triangular_solve | solution.py:19
  308.7 0.5 fusion.9
  309.2 0.5 convolution_subtract_fusion
  309.7 0.5 fusion.8
  310.3 1.4 convolution_multiply_fusion
  311.7 0.5 copy.140
  312.3 29.0 %all_to_all.27 = f32[3,256,256]{2,0,1:T(4,128)S(1)} all-to-all(f32[3,256,256]{2,0,1:T(4,128)S(1)} %copy.140), channel_id=1, replica_groups=mesh['pipe'=4,'dp'=8] {'dp'}, dimensions={1} | all-to-all | bytes 1572864 | tf_op jit(solution)/shard_map/all_to_all | solution.py:82
  341.3 0.2 copy.141
  341.4 1.0 copy.142
  342.4 0.3 all-gather.8.cloned.1.call-start
  342.7 0.7 fusion.26
  343.4 40.9 %all-gather.6.cloned.1.call-done = f32[96,32,256]{2,1,0:T(8,128)} async-done(((f32[24,32,256]{2,1,0:T(8,128)}), f32[96,32,256]{2,1,0:T(8,128)}) %all-gather.6.cloned.1.call-update) | async-done | bytes 3145744 | tf_op jit(solution)/shard_map/all_gather | solution.py:84
  384.4 4.7 %fusion = f32[12,32,256]{2,0,1:T(8,128)S(1)} fusion(f32[96,32,256]{2,1,0:T(8,128)} %all-gather.6.cloned.1.call-done, s32[12]{0:T(128)S(1)} %fusion.26), kind=kOutput, calls=%fused_computation.3 | convolution fusion | flops 113247360 | bytes 3538992 | tf_op jit(solution)/shard_map/bm,mrc->brc/dot_general | solution.py:85
  389.0 1.0 copy.144
  390.0 38.4 %all-gather.8.cloned.1.call-done = f32[12,256,256]{2,1,0:T(8,128)} async-done(((f32[12,32,256]{2,1,0:T(8,128)}), f32[12,256,256]{2,1,0:T(8,128)}) %all-gather.8.cloned.1.call-update) | async-done | bytes 3145744 | tf_op jit(solution)/shard_map/all_gather | solution.py:86
  428.4 12.5 %fusion.31 = f32[12,256,512]{2,1,0:T(8,128)} fusion(f32[12,256,256]{2,1,0:T(8,128)} %all-gather.8.cloned.1.call-done, f32[12,256,512]{2,1,0:T(8,128)} %bitcast.77), kind=kOutput, calls=%fused_computation.66 | convolution fusion | flops 4831838208 | bytes 15728640 | tf_op jit(solution)/shard_map/brk,bkc->brc/dot_general | solution.py:88
  (29 shorter events, 0.3 us)
Async XLA Ops:
  7.2 50.8 %reduce-scatter.2.cloned.1.call-start = ((), (), s32[]{:S(2)}) async-start(), calls=%async_computation.3 | async-start | bytes 3538944 | tf_op jit(solution)/shard_map/reduce_scatter | solution.py:59
  14.7 43.3 %copy-start.2 = (s32[4,12]{1,0:T(4,128)S(1)}, s32[4,12]{1,0:T(4,128)}, u32[]{:S(2)}) copy-start(s32[4,12]{1,0:T(4,128)} %param.5) | copy-start | bytes 580
  14.7 75.2 %all-gather.4.cloned.1.call-start = ((), (), s32[]{:S(2)}) async-start(), calls=%async_computation.4 | async-start | bytes 1966080 | tf_op jit(solution)/shard_map/all_gather | solution.py:65
  58.4 34.2 %copy-start.3 = (s32[4,12]{1,0:T(4,128)}, s32[4,12]{1,0:T(4,128)S(1)}, u32[]{:S(2)}) copy-start(s32[4,12]{1,0:T(4,128)S(1)} %reshape.93) | copy-start | bytes 580
  93.7 25.6 %all-to-all-start = ((f32[24,32,256]{2,1,0:T(8,128)}), f32[24,32,256]{2,1,0:T(8,128)S(1)}, u32[]{:S(2)}, u32[]{:S(2)}) async-start(f32[24,32,256]{2,1,0:T(8,128)} %copy.127), calls=%async_computation.1 | async-start | bytes 1572864 | tf_op jit(solution)/shard_map/all_to_all | solution.py:78
  98.3 286.0 %all-gather.6.cloned.1.call-start = ((), (), s32[]{:S(2)}) async-start(), calls=%async_computation.5 | async-start | bytes 3932160 | tf_op jit(solution)/shard_map/all_gather | solution.py:84
  139.4 0.5 copy-start.4
  140.4 102.9 %copy-start.1 = (pred[256,256]{1,0:T(8,128)(4,1)S(1)}, pred[256,256]{1,0:T(8,128)(4,1)}, u32[]{:S(2)}) copy-start(pred[256,256]{1,0:T(8,128)(4,1)} %iota_compare_fusion.1) | copy-start | bytes 196612
  141.2 102.3 %copy-start.6 = (s32[2]{0:T(128)S(1)}, s32[2]{0:T(128)}, u32[]{:S(2)}) copy-start(s32[2]{0:T(128)} %iota_multiply_fusion) | copy-start | bytes 28
  176.5 132.2 %copy-start = (f32[128,256]{1,0:T(8,128)S(1)}, f32[128,256]{1,0:T(8,128)}, u32[]{:S(2)}) copy-start(f32[128,256]{1,0:T(8,128)} %copy.135) | copy-start | bytes 393220
  243.3 67.0 %copy-start.5 = (f32[3]{0:T(128)S(1)}, f32[3]{0:T(128)}, u32[]{:S(2)}) copy-start(f32[3]{0:T(128)} %get-tuple-element.21) | copy-start | bytes 40
  342.4 86.0 %all-gather.8.cloned.1.call-start = ((), (), s32[]{:S(2)}) async-start(), calls=%async_computation.6 | async-start | bytes 3538944 | tf_op jit(solution)/shard_map/all_gather | solution.py:86
Sparse Core Ops, SparseCore 0:
  14.9 43.0 reduce-scatter.1
  59.8 30.0 all-gather.3
  342.5 41.7 all-gather.5
  390.1 38.1 all-gather.7
where the time goes:
time: 448 us; the launch traced here: 447 us
  waiting for transfers between devices  172 us (38%)
  other arithmetic  165 us (37%)
  local copies, waits for them, and re-layouts  37.5 us (8%)
  blocking collectives  29 us (6%)
  matrix products  24.2 us (5%)
  between operations  14.1 us (3%)
  starting transfers between devices  5.21 us (1%)
    another operation x9, other arithmetic, invert_blocks(): cholesky_lower = jnp.linalg.cholesky(shifted)  102 us
    another operation x4, other arithmetic, invert_blocks(): lax.linalg.triangular_solve(cholesky_lower, identity_stack, left_side=Tru...  61.1 us
    reduce_scatter x1, waiting for transfers between devices, shards(): lax.psum_scatter(block_terms.reshape(row_share * lax.axis_size('dp'), nbl...  43.2 us
    all_gather x1, waiting for transfers between devices, shards(): returned = lax.all_gather(held_rows, 'pipe', axis=0, tiled=True)  40.9 us
    all_gather x1, waiting for transfers between devices, shards(): inverse = lax.all_gather(own_rows, 'dp', axis=1, tiled=True)  38.4 us
    all_gather x1, waiting for transfers between devices, shards(): lax.all_gather(my_rows, 'pipe', axis=0, tiled=True)  31.6 us
    all_to_all x1, blocking collectives, shards(): lax.all_to_all(inverted, 'dp', split_axis=1, concat_axis=0, tiled=True)  29 us
    all_to_all x1, waiting for transfers between devices, shards(): lax.all_to_all(padded, 'dp', split_axis=0, concat_axis=1, tiled=True)  17.8 us
  transfers between devices with their start and end apart: 5, of which 5 were waited for; matrix products, arithmetic and copies ran while one was open for 1% of the time, Pallas kernels for 0%

commit v1 on v0

--- a/solution.py
+++ b/solution.py
@@ -83,7 +83,8 @@
     held_rows = spread_rows[:HOST]
     returned = lax.all_gather(held_rows, "pipe", axis=0, tiled=True)
     own_rows = jnp.einsum("bm,mrc->brc", pick_back, returned, precision=lax.Precision.HIGHEST)
-    inverse = lax.all_gather(own_rows, "dp", axis=1, tiled=True)
+    high = jax.lax.all_gather(own_rows, "dp")
+    inverse = jnp.concatenate(high, 1)
     grad_blocks = grad.reshape(nblocks, BLK, grad.shape[1])
     precond = jnp.einsum("brk,bkc->brc", inverse, grad_blocks, precision=lax.Precision.HIGHEST)
     return (precond.reshape(feature_count, grad.shape[1]), held_rows[None])

time: 448 us -> 448 us (level)
  no operation moved by 1% of the time
where the time goes in v1:
time: 448 us; the launch traced here: 447 us
  waiting for transfers between devices  172 us (38%)
  other arithmetic  165 us (37%)
  local copies, waits for them, and re-layouts  39.6 us (9%)
  blocking collectives  29 us (6%)
  matrix products  22.1 us (5%)
  between operations  14.1 us (3%)
  starting transfers between devices  5.2 us (1%)
    another operation x9, other arithmetic, invert_blocks(): cholesky_lower = jnp.linalg.cholesky(shifted)  102 us
    another operation x4, other arithmetic, invert_blocks(): lax.linalg.triangular_solve(cholesky_lower, identity_stack, left_side=Tru...  61.1 us
    reduce_scatter x1, waiting for transfers between devices, shards(): lax.psum_scatter(block_terms.reshape(row_share * lax.axis_size('dp'), nbl...  43.2 us
    all_gather x1, waiting for transfers between devices, shards(): returned = lax.all_gather(held_rows, 'pipe', axis=0, tiled=True)  40.9 us
    all_gather x1, waiting for transfers between devices, shards(): high = jax.lax.all_gather(own_rows, 'dp')  38.4 us
    all_gather x1, waiting for transfers between devices, shards(): lax.all_gather(my_rows, 'pipe', axis=0, tiled=True)  31.6 us
    all_to_all x1, blocking collectives, shards(): lax.all_to_all(inverted, 'dp', split_axis=1, concat_axis=0, tiled=True)  29 us
    all_to_all x1, waiting for transfers between devices, shards(): lax.all_to_all(padded, 'dp', split_axis=0, concat_axis=1, tiled=True)  17.9 us
  transfers between devices with their start and end apart: 5, of which 5 were waited for; matrix products, arithmetic and copies ran while one was open for 1% of the time, Pallas kernels for 0%

profile of v1, /device:TPU:0, one launch (start us, length us, event | category | flops | bytes accessed | tf_op | source)
XLA Modules:
  0.0 447.5 jit_solution(5242161687880719674)
XLA Ops:
  7.2 1.7 copy.108
  8.9 2.3 fusion.29
  11.2 3.5 copy.110
  14.8 43.2 %reduce-scatter.2.cloned.1.call-done = f32[32,3072]{1,0:T(8,128)} async-done(((f32[256,3072]{1,0:T(8,128)}), f32[32,3072]{1,0:T(8,128)}) %reduce-scatter.2.cloned.1.call-update) | async-done | bytes 393232 | tf_op jit(solution)/shard_map/reduce_scatter | solution.py:59
  58.0 0.1 eq.76
  58.1 0.2 convert_reduce_fusion
  58.3 0.1 reshape.99
  58.4 31.6 %all-gather.5.cloned.1.call-done = f32[128,3072]{1,0:T(8,128)} async-done(((f32[32,3072]{1,0:T(8,128)}), f32[128,3072]{1,0:T(8,128)}) %all-gather.5.cloned.1.call-update) | async-done | bytes 1572880 | tf_op jit(solution)/shard_map/all_gather | solution.py:65
  90.0 1.7 reshape.101
  91.7 0.9 convolution_bitcast_fusion
  92.6 1.1 copy.112
  93.7 4.6 %all-to-all-start = ((f32[24,32,256]{2,1,0:T(8,128)}), f32[24,32,256]{2,1,0:T(8,128)S(1)}, u32[]{:S(2)}, u32[]{:S(2)}) async-start(f32[24,32,256]{2,1,0:T(8,128)} %copy.112), calls=%async_computation.1 | async-start | bytes 1572864 | tf_op jit(solution)/shard_map/all_to_all | solution.py:78
  98.3 0.2 all-gather.7.cloned.1.call-start
  98.6 0.7 copy.120
  99.4 0.1 copy.122
  99.5 0.5 iota_multiply_fusion
  100.0 0.1 convert_reduce_fusion.1
  100.1 0.6 iota_compare_fusion.2
  100.8 0.6 iota_compare_fusion.1
  101.4 17.9 %all-to-all-done = f32[24,32,256]{2,1,0:T(8,128)S(1)} async-done(((f32[24,32,256]{2,1,0:T(8,128)}), f32[24,32,256]{2,1,0:T(8,128)S(1)}, u32[]{:S(2)}, u32[]{:S(2)}) %all-to-all-start) | async-done | bytes 786464 | tf_op jit(solution)/shard_map/all_to_all | solution.py:78
  119.3 0.1 broadcast_multiply_fusion
  119.3 0.1 copy.113
  119.4 16.4 %copy.114 = f32[3,256,256]{0,2,1:T(8,128)} copy(f32[3,256,256]{2,1,0:T(8,128)S(1)} %bitcast.81) | data formatting | bytes 1572864 | tf_op jit(solution)/shard_map/div | solution.py:78
  135.8 0.3 copy.115
  136.1 2.3 gather_fusion
  138.4 0.1 reduce_sum.28
  138.5 0.6 subtract_add_fusion
  139.1 0.5 copy-done.5
  139.6 0.1 multiply_add_fusion
  139.7 0.3 copy.116
  140.0 0.8 fusion.3
  140.8 35.2 %custom-call.16 = f32[3,128,128]{2,1,0:T(8,128)S(1)} custom-call(f32[3,128,128]{2,1,0:T(8,128)S(1)} %cholesky.122), custom_call_target="Cholesky" | custom-call | tf_op jit(solution)/shard_map/jit(cholesky)/cholesky | solution.py:17
  176.0 0.1 cholesky.117
  176.1 0.8 select_bitcast_fusion
  176.9 29.5 %custom-call.17 = f32[3,1,128,128]{2,3,1,0:T(8,128)S(1)} custom-call(f32[3,1,128,128]{3,2,1,0:T(8,128)S(1)} %select_bitcast_fusion), custom_call_target="InvertDiagBlocksLowerTriangular" | custom-call | tf_op jit(solution)/shard_map/jit(cholesky)/cholesky | solution.py:17
  206.4 0.4 constant_dynamic-update-slice_fusion.1
  206.7 0.5 convolution_subtract_fusion.1
  207.3 35.4 %custom-call.18 = f32[3,128,128]{2,1,0:T(8,128)S(1)} custom-call(f32[3,128,128]{2,1,0:T(8,128)S(1)} %convolution_subtract_fusion.1), custom_call_target="Cholesky" | custom-call | tf_op jit(solution)/shard_map/jit(cholesky)/cholesky | solution.py:17
  242.7 0.1 compare_reduce_fusion
  242.9 0.2 select_select_fusion
  243.1 0.1 triangular_solve.69
  243.1 5.2 %while.1 = (s32[]{:T(128)}, f32[3,256,256]{2,1,0:T(8,128)S(1)}, s32[2,2]{1,0:T(2,128)S(1)}, f32[2,3,128,128]{3,2,0,1:T(8,128)}, s32[]{:T(128)}) while((s32[]{:T(128)}, f32[3,256,256]{2,1,0:T(8,128)S(1)}, s32[2,2]{1,0:T(2,128)S(1)}, f32[2,3,128,128]{3,2,0,1:T(8,128)}, s32[]{:T(128)}) %tuple.29), condition=%wide.while_cond, body=%wide.while_body.sunk | while | flops 2 | bytes 394849 | solution.py:19
  243.2 0.6 fusion.42
  243.7 2.0 bitcast_dynamic-update-slice_fusion.2
  245.7 0.6 fusion.42
  246.3 2.0 bitcast_dynamic-update-slice_fusion.2
  248.3 59.8 %custom-call.19 = f32[3,2,128,128]{2,3,1,0:T(8,128)S(1)} custom-call(f32[3,2,128,128]{3,2,1,0:T(8,128)} %bitcast.90), custom_call_target="InvertDiagBlocksLowerTriangular" | custom-call | tf_op jit(solution)/shard_map/triangular_solve | solution.py:19
  308.1 0.5 fusion.7
  308.6 0.5 convolution_subtract_fusion
  309.1 0.5 fusion.6
  309.7 1.4 convolution_multiply_fusion
  311.1 0.5 copy.125
  311.7 29.0 %all_to_all.27 = f32[3,256,256]{2,0,1:T(4,128)S(1)} all-to-all(f32[3,256,256]{2,0,1:T(4,128)S(1)} %copy.125), channel_id=1, replica_groups=mesh['pipe'=4,'dp'=8] {'dp'}, dimensions={1} | all-to-all | bytes 1572864 | tf_op jit(solution)/shard_map/all_to_all | solution.py:82
  340.7 0.2 copy.126
  340.8 0.1 copy.127
  340.9 1.3 copy.128
  342.2 0.3 all-gather.9.cloned.1.call-start
  342.6 0.7 fusion.25
  343.3 40.9 %all-gather.7.cloned.1.call-done = f32[96,32,256]{2,0,1:T(8,128)} async-done(((f32[24,32,256]{2,0,1:T(8,128)}), f32[96,32,256]{2,0,1:T(8,128)}) %all-gather.7.cloned.1.call-update) | async-done | bytes 3145744 | tf_op jit(solution)/shard_map/all_gather | solution.py:84
  384.2 3.0 fusion.20
  387.2 1.0 copy.129
  388.2 38.4 %all-gather.9.cloned.1.call-done = f32[96,32,256]{2,1,0:T(8,128)} async-done(((f32[12,32,256]{2,1,0:T(8,128)}), f32[96,32,256]{2,1,0:T(8,128)}) %all-gather.9.cloned.1.call-update) | async-done | bytes 3145744 | tf_op jit(solution)/shard_map/all_gather | solution.py:86
  426.6 2.3 copy.130
  428.8 12.1 %fusion.30 = f32[12,256,512]{2,1,0:T(8,128)} fusion(f32[12,256,256]{2,1,0:T(8,128)S(1)} %bitcast.80, f32[12,256,512]{2,1,0:T(8,128)} %bitcast.83), kind=kOutput, calls=%fused_computation.65 | convolution fusion | flops 4831838208 | bytes 15728640 | tf_op jit(solution)/shard_map/brk,bkc->brc/dot_general | solution.py:89
  (33 shorter events, 0.3 us)
Async XLA Ops:
  7.2 50.8 %reduce-scatter.2.cloned.1.call-start = ((), (), s32[]{:S(2)}) async-start(), calls=%async_computation.3 | async-start | bytes 3538944 | tf_op jit(solution)/shard_map/reduce_scatter | solution.py:59
  14.7 43.3 %copy-start.3 = (s32[4,12]{1,0:T(4,128)S(1)}, s32[4,12]{1,0:T(4,128)}, u32[]{:S(2)}) copy-start(s32[4,12]{1,0:T(4,128)} %param.5) | copy-start | bytes 580
  14.8 75.2 %all-gather.5.cloned.1.call-start = ((), (), s32[]{:S(2)}) async-start(), calls=%async_computation.4 | async-start | bytes 1966080 | tf_op jit(solution)/shard_map/all_gather | solution.py:65
  58.4 34.2 %copy-start.4 = (s32[4,12]{1,0:T(4,128)}, s32[4,12]{1,0:T(4,128)S(1)}, u32[]{:S(2)}) copy-start(s32[4,12]{1,0:T(4,128)S(1)} %reshape.99) | copy-start | bytes 580
  93.7 25.6 %all-to-all-start = ((f32[24,32,256]{2,1,0:T(8,128)}), f32[24,32,256]{2,1,0:T(8,128)S(1)}, u32[]{:S(2)}, u32[]{:S(2)}) async-start(f32[24,32,256]{2,1,0:T(8,128)} %copy.112), calls=%async_computation.1 | async-start | bytes 1572864 | tf_op jit(solution)/shard_map/all_to_all | solution.py:78
  98.3 285.9 %all-gather.7.cloned.1.call-start = ((), (), s32[]{:S(2)}) async-start(), calls=%async_computation.5 | async-start | bytes 3932160 | tf_op jit(solution)/shard_map/all_gather | solution.py:84
  139.1 0.5 copy-start.5
  140.0 102.9 %copy-start.2 = (pred[256,256]{1,0:T(8,128)(4,1)S(1)}, pred[256,256]{1,0:T(8,128)(4,1)}, u32[]{:S(2)}) copy-start(pred[256,256]{1,0:T(8,128)(4,1)} %iota_compare_fusion.1) | copy-start | bytes 196612
  140.8 102.3 %copy-start.7 = (s32[2]{0:T(128)S(1)}, s32[2]{0:T(128)}, u32[]{:S(2)}) copy-start(s32[2]{0:T(128)} %iota_multiply_fusion) | copy-start | bytes 28
  176.1 132.0 %copy-start.1 = (f32[128,256]{1,0:T(8,128)S(1)}, f32[128,256]{1,0:T(8,128)}, u32[]{:S(2)}) copy-start(f32[128,256]{1,0:T(8,128)} %copy.120) | copy-start | bytes 393220
  242.9 66.8 %copy-start.6 = (f32[3]{0:T(128)S(1)}, f32[3]{0:T(128)}, u32[]{:S(2)}) copy-start(f32[3]{0:T(128)} %get-tuple-element.21) | copy-start | bytes 40
  340.9 47.3 %copy-start = (f32[8,3,32,256]{3,2,1,0:T(8,128)}, f32[8,3,32,256]{3,2,1,0:T(8,128)S(1)}, u32[]{:S(2)}) copy-start(f32[8,3,32,256]{3,2,1,0:T(8,128)S(1)} %copy.127) | copy-start | bytes 2359300
  342.2 84.3 %all-gather.9.cloned.1.call-start = ((), (), s32[]{:S(2)}) async-start(), calls=%async_computation.6 | async-start | bytes 3538944 | tf_op jit(solution)/shard_map/all_gather | solution.py:86
Sparse Core Ops, SparseCore 0:
  14.9 43.0 reduce-scatter.1
  59.8 30.0 all-gather.4
  342.4 41.7 all-gather.6
  388.3 38.2 all-gather.8
